TPU v7x, 32 devices: a whole 2x2x4 slice. The times are simulated.
32 devices in a mesh: layer: 2 (over x), row: 4 (over z), col: 4 (over y, core).
Axes of the slice: x: 2, y: 2, z: 4, core: 2. Of those that a mesh axis runs over, the one named last changes fastest.
Arguments:
- left_matrix: float32 [2, 1024, 16384], P(None, 'row', 'col'), may hold values from -6 to 6
- right_matrix: float32 [2, 16384, 512], P(None, 'row', 'col'), may hold values from -0.03125 to 0.03125
Outputs:
- product: float32 [2, 1024, 512], P(None, 'row', 'col')
All inputs are finite; a program needn't handle non-finite values.
Results may differ from a plain program's by a relative error of at most 0.000071.
Values sent between devices are 32-bit elements; how exact they have to be, the bound alone decides.
A program may use at most 128 MiB of HBM per device.

v0:
```python
import jax
import jax.numpy as jnp
from jax import lax
from jax.sharding import PartitionSpec as P


def gauss_fold(right_whole, site_rows, cols_out):
    right_real = right_whole[0]
    right_imag = right_whole[1]
    right_total = right_real + right_imag
    highest = lax.Precision.HIGHEST
    empty = jnp.zeros((site_rows, cols_out), jnp.float32)

    def accumulate(totals, segment, offset):
        left_real = segment[0]
        left_imag = segment[1]
        first_term = jnp.dot(
            left_real, right_real, precision=highest, preferred_element_type=jnp.float32
        )
        second_term = jnp.dot(
            left_imag, right_imag, precision=highest, preferred_element_type=jnp.float32
        )
        third_term = jnp.dot(
            left_real + left_imag,
            right_total,
            precision=highest,
            preferred_element_type=jnp.float32,
        )
        return (first_term, second_term, third_term)

    return (accumulate, (empty, empty, empty))


def combine_terms(totals):
    first_term, second_term, third_term = totals
    return jnp.stack([first_term - second_term, third_term - first_term - second_term])


def local(left_matrix, right_matrix):
    layers = lax.axis_size("layer")
    layer_index = lax.axis_index("layer")
    local_rows = left_matrix.shape[1]
    local_cols = right_matrix.shape[2]
    left_width = left_matrix.shape[2]
    right_height = right_matrix.shape[1]
    share_width = left_width // layers
    group_count = right_height // left_width
    left_own = lax.dynamic_slice_in_dim(left_matrix, layer_index * share_width, share_width, 2)
    right_view = right_matrix.reshape(2, group_count, layers, share_width, local_cols)
    right_own = lax.dynamic_slice_in_dim(right_view, layer_index, 1, 2)
    right_own = right_own.reshape(2, group_count * share_width, local_cols)
    right_whole = lax.all_gather(right_own, "row", axis=1, tiled=True)
    accumulate, initial = gauss_fold(right_whole, local_rows, local_cols)
    totals = accumulate(initial, lax.all_gather(left_own, "col", axis=2, tiled=True), jnp.int32(0))
    partial_product = combine_terms(totals)
    product = lax.psum(partial_product, "layer")
    return product


def solution(mesh):
    in_specs = (P(None, "row", "col"), P(None, "row", "col"))
    out_specs = P(None, "row", "col")
    return jax.shard_map(local, mesh=mesh, in_specs=in_specs, out_specs=out_specs, check_vma=False)
```

profile of v0, /device:TPU:0, one launch (start us, length us, event | category | flops | bytes accessed | tf_op | source)
XLA Modules:
  0.0 329.2 jit_solution(11281705026312441378)
XLA Ops:
  6.5 0.0 all-gather.6.cloned.1.call-start
  6.5 3.1 constant_dynamic-slice_fusion
  9.6 0.0 all-gather.6.cloned.1.call-update
  9.6 0.0 all-gather.4.cloned.1.call-start
  9.7 4.7 %constant_dynamic-slice_fusion.1 = f32[2,256,2048]{2,1,0:T(8,128)} fusion(f32[2,256,4096]{2,1,0:T(8,128)} %param.2, s32[]{:T(128)S(6)} %select_n.6), kind=kLoop, calls=%fused_computation.25 | loop fusion | bytes 8388612 | tf_op jit(solution)/shard_map/dynamic_slice | solution.py:48
  14.3 0.0 all-gather.4.cloned.1.call-update
  14.3 0.0 all-reduce.2.cloned.1.call-start
  14.4 147.7 %all-gather.6.cloned.1.call-done = f32[2,1,1,8192,128]{4,3,2,0,1:T(8,128)} async-done(((f32[2,1,1,2048,128]{4,3,2,0,1:T(8,128)}), f32[2,1,1,8192,128]{4,3,2,0,1:T(8,128)}) %all-gather.6.cloned.1.call-update) | async-done | bytes 8388624 | tf_op jit(solution)/shard_map/all_gather | solution.py:52
  162.1 105.7 %all-gather.4.cloned.1.call-done = f32[2,256,8192]{2,1,0:T(8,128)} async-done(((f32[2,256,2048]{2,1,0:T(8,128)}), f32[2,256,8192]{2,1,0:T(8,128)}) %all-gather.4.cloned.1.call-update) | async-done | bytes 16777232 | tf_op jit(solution)/shard_map/all_gather | solution.py:54
  267.8 0.0 copy-start
  267.8 9.9 %fusion.4 = f32[256,128]{1,0:T(8,128)S(1)} fusion(f32[2,256,8192]{2,1,0:T(8,128)} %all-gather.4.cloned.1.call-done, f32[2,1,1,8192,128]{4,3,2,0,1:T(8,128)} %all-gather.6.cloned.1.call-done), kind=kOutput, calls=%fused_computation.4 | convolution fusion | flops 3221225472 | bytes 12713984 | tf_op jit(solution)/shard_map/dot_general | solution.py:17
  277.7 9.8 %fusion.2 = f32[256,128]{1,0:T(8,128)S(1)} fusion(f32[2,256,8192]{2,1,0:T(8,128)} %all-gather.4.cloned.1.call-done, f32[2,1,1,8192,128]{4,3,2,0,1:T(8,128)} %all-gather.6.cloned.1.call-done), kind=kOutput, calls=%fused_computation.2 | convolution fusion | flops 3221225472 | bytes 12713984 | tf_op jit(solution)/shard_map/dot_general | solution.py:20
  287.6 0.0 copy-done
  287.6 9.2 %fusion.29 = f32[1,256,128]{2,1,0:T(8,128)S(1)} fusion(f32[256,128]{1,0:T(8,128)S(1)} %fusion.2, f32[256,128]{1,0:T(8,128)S(1)} %fusion.4, f32[2,1,1,8192,128]{4,3,2,0,1:T(8,128)} %all-gather.6.cloned.1.call-done, f32[2,256,8192]{2,1,0:T(8,128)S(1)} %copy-done), kind=kOutput, calls=%fused_computation.21 | convolution fusion | flops 3224436736 | bytes 25559040 | tf_op jit(solution)/shard_map/dot_general | solution.py:23
  296.8 0.7 pad_maximum_fusion
  297.5 0.0 all-reduce.2.cloned.1.call-update
  297.5 23.4 %all-reduce.2.cloned.1.call-done = f32[2,256,128]{2,1,0:T(8,128)} async-done(((f32[2,256,128]{2,1,0:T(8,128)}), f32[2,256,128]{2,1,0:T(8,128)}) %all-reduce.2.cloned.1.call-update) | async-done | bytes 262160 | tf_op jit(solution)/shard_map/psum | solution.py:56
  321.0 1.7 copy.4
  (1 shorter events, 0.0 us)
Async XLA Ops:
  6.5 155.6 %all-gather.6.cloned.1.call-start = ((), (), s32[]{:S(2)}) async-start(), calls=%async_computation.2 | async-start | bytes 10485760 | tf_op jit(solution)/shard_map/all_gather | solution.py:52
  9.6 258.2 %all-gather.4.cloned.1.call-start = ((), (), s32[]{:S(2)}) async-start(), calls=%async_computation | async-start | bytes 20971520 | tf_op jit(solution)/shard_map/all_gather | solution.py:54
  14.3 306.6 %all-reduce.2.cloned.1.call-start = ((), (), s32[]{:S(2)}) async-start(), calls=%async_computation.1 | async-start | bytes 524288 | tf_op jit(solution)/shard_map/psum | solution.py:56
  267.8 19.8 %copy-start = (f32[2,256,8192]{2,1,0:T(8,128)S(1)}, f32[2,256,8192]{2,1,0:T(8,128)}, u32[]{:S(2)}) copy-start(f32[2,256,8192]{2,1,0:T(8,128)} %all-gather.4.cloned.1.call-done) | copy-start | bytes 50331652
Sparse Core Ops, SparseCore 0:
  9.7 152.3 all-gather.5
  163.7 104.0 all-gather.3
  297.7 23.2 all-reduce.1
where the time goes:
time: 329 us
  waiting for transfers between devices  277 us (84%)
  matrix products  28.9 us (9%)
  between operations  13.2 us (4%)
  local copies, waits for them, and re-layouts  9.38 us (3%)
    all_gather x1, waiting for transfers between devices, local(): right_whole = lax.all_gather(right_own, 'row', axis=1, tiled=True)  148 us
    all_gather x1, waiting for transfers between devices, local(): lax.all_gather(left_own, 'col', axis=2, tiled=True)  106 us
    psum x1, waiting for transfers between devices, local(): product = lax.psum(partial_product, 'layer')  23.4 us
    dot_general x1, matrix products, accumulate(): jnp.dot(left_real, right_real, precision=highest, preferred_element_type=...  9.94 us
    dot_general x1, matrix products, accumulate(): jnp.dot(left_imag, right_imag, precision=highest, preferred_element_type=...  9.81 us
    dot_general x1, matrix products, accumulate(): jnp.dot(left_real + left_imag, right_total, precision=highest, preferred_...  9.2 us
  transfers between devices with their start and end apart: 3, of which 3 were waited for; matrix products, arithmetic and copies ran while one was open for 1% of the time, Pallas kernels for 0%

commit v1 on v0

--- a/solution.py
+++ b/solution.py
@@ -49,7 +49,15 @@
     right_view = right_matrix.reshape(2, group_count, layers, share_width, local_cols)
     right_own = lax.dynamic_slice_in_dim(right_view, layer_index, 1, 2)
     right_own = right_own.reshape(2, group_count * share_width, local_cols)
-    right_whole = lax.all_gather(right_own, "row", axis=1, tiled=True)
+    dev_n = lax.axis_size("row")
+    raw_out = [(w - 1, w) for w in range(1, dev_n)] + [(dev_n - 1, 0)]
+    field_out = right_own
+    series = [field_out]
+    for _ in range(dev_n - 1):
+        field_out = lax.ppermute(field_out, "row", perm=raw_out)
+        series += [field_out]
+    plain = jnp.concatenate([*reversed(series)], axis=1)
+    right_whole = jnp.roll(plain, (lax.axis_index("row") + 1) * field_out.shape[1], axis=1)
     accumulate, initial = gauss_fold(right_whole, local_rows, local_cols)
     totals = accumulate(initial, lax.all_gather(left_own, "col", axis=2, tiled=True), jnp.int32(0))
     partial_product = combine_terms(totals)

time: 329 us -> 240 us (0.73)
  waiting for transfers between devices: 277 us -> 166 us
  local copies, waits for them, and re-layouts: 9.38 us -> 27.8 us
    all_gather x1 -> x0, waiting for transfers between devices: 148 us -> none  [local(): right_whole = lax.all_gather(right_own, 'row', axis=1, tiled=True)]
    ppermute x0 -> x3, waiting for transfers between devices: none -> 144 us  [local(): field_out = lax.ppermute(field_out, 'row', perm=raw_out)]
    all_gather x1, waiting for transfers between devices: 106 us -> 0.01 us  [local(): lax.all_gather(left_own, 'col', axis=2, tiled=True)]
    unnamed x3 -> x12, local copies, waits for them, and re-layouts: 1.67 us -> 19.8 us
  transfers between devices with their start and end apart: 3 -> 5, of which waited for: 3 -> 4; matrix products, arithmetic and copies ran while one was open for 1% -> 9% of each run, Pallas kernels for 0% -> 0%
where the time goes in v1:
time: 240 us
  waiting for transfers between devices  166 us (69%)
  matrix products  29.3 us (12%)
  local copies, waits for them, and re-layouts  27.8 us (12%)
  between operations  13.5 us (6%)
  starting transfers between devices  3.15 us (1%)
    ppermute x3, waiting for transfers between devices, local(): field_out = lax.ppermute(field_out, 'row', perm=raw_out)  144 us
    psum x1, waiting for transfers between devices, local(): product = lax.psum(partial_product, 'layer')  21.2 us
    unnamed x12, local copies, waits for them, and re-layouts  19.8 us
    dot_general x1, matrix products, accumulate(): jnp.dot(left_real, right_real, precision=highest, preferred_element_type=...  9.94 us
    dot_general x1, matrix products, accumulate(): jnp.dot(left_imag, right_imag, precision=highest, preferred_element_type=...  9.82 us
    dot_general x1, matrix products, accumulate(): jnp.dot(left_real + left_imag, right_total, precision=highest, preferred_...  9.55 us
  transfers between devices with their start and end apart: 5, of which 4 were waited for; matrix products, arithmetic and copies ran while one was open for 9% of the time, Pallas kernels for 0%

profile of v1, /device:TPU:0, one launch (start us, length us, event | category | flops | bytes accessed | tf_op | source)
XLA Modules:
  0.0 240.1 jit_solution(14352232666211421458)
XLA Ops:
  6.5 0.0 all-gather.2.cloned.1.call-start
  6.5 4.8 %constant_dynamic-slice_fusion = f32[2,256,2048]{2,1,0:T(8,128)} fusion(f32[2,256,4096]{2,1,0:T(8,128)} %param.2, s32[]{:T(128)S(6)} %select_n.19), kind=kLoop, calls=%fused_computation.36 | loop fusion | bytes 8388612 | tf_op jit(solution)/shard_map/dynamic_slice | solution.py:48
  11.3 0.0 all-gather.2.cloned.1.call-update
  11.3 0.0 all-reduce.2.cloned.1.call-start
  11.4 1.7 dynamic-slice_bitcast_fusion
  13.1 3.1 %collective-permute-start = (f32[2,2048,128]{2,1,0:T(8,128)S(1)}, f32[2,2048,128]{2,1,0:T(8,128)S(1)}, u32[]{:S(2)}, u32[]{:S(2)}) collective-permute-start(f32[2,2048,128]{2,1,0:T(8,128)S(1)} %dynamic-slice_bitcast_fusion), channel_id=1, source_target_pairs={{0,4},{4,8},{8,12},{12,0},{1,5},{5,9},{9,13},{13,1},{2,6},{6,10},{... | collective-permute-start | bytes 6291464 | tf_op jit(solution)/shard_map/ppermute | solution.py:57
  16.2 47.7 %collective-permute-done = f32[2,2048,128]{2,1,0:T(8,128)S(1)} collective-permute-done((f32[2,2048,128]{2,1,0:T(8,128)S(1)}, f32[2,2048,128]{2,1,0:T(8,128)S(1)}, u32[]{:S(2)}, u32[]{:S(2)}) %collective-permute-start) | collective-permute-done | bytes 2097184 | tf_op jit(solution)/shard_map/ppermute | solution.py:57
  63.9 0.0 collective-permute-start.1
  63.9 48.7 %collective-permute-done.1 = f32[2,2048,128]{2,1,0:T(8,128)} collective-permute-done((f32[2,2048,128]{2,1,0:T(8,128)S(1)}, f32[2,2048,128]{2,1,0:T(8,128)}, u32[]{:S(2)}, u32[]{:S(2)}) %collective-permute-start.1) | collective-permute-done | bytes 2097184 | tf_op jit(solution)/shard_map/ppermute | solution.py:57
  112.6 0.0 collective-permute-start.2
  112.6 0.0 copy-start.1
  112.6 48.0 %collective-permute-done.2 = f32[2,2048,128]{2,1,0:T(8,128)} collective-permute-done((f32[2,2048,128]{2,1,0:T(8,128)}, f32[2,2048,128]{2,1,0:T(8,128)}, u32[]{:S(2)}, u32[]{:S(2)}) %collective-permute-start.2) | collective-permute-done | bytes 2097184 | tf_op jit(solution)/shard_map/ppermute | solution.py:57
  160.6 3.1 %constant_dynamic-update-slice_fusion.7 = f32[2,16384,128]{2,1,0:T(8,128)} fusion(f32[2,2048,128]{2,1,0:T(8,128)} %collective-permute-done.2), kind=kLoop, calls=%fused_computation.32 | loop fusion | bytes 4194304
  163.7 3.0 %constant_dynamic-update-slice_fusion.6 = f32[2,16384,128]{2,1,0:T(8,128)} fusion(f32[2,16384,128]{2,1,0:T(8,128)} %constant_dynamic-update-slice_fusion.7, f32[2,2048,128]{2,1,0:T(8,128)} %collective-permute-done.1), kind=kLoop, calls=%fused_computation.31 | loop fusion | bytes 4194304
  166.7 1.5 constant_dynamic-update-slice_fusion.5
  168.2 3.0 %constant_dynamic-update-slice_fusion.4 = f32[2,16384,128]{2,1,0:T(8,128)} fusion(f32[2,16384,128]{2,1,0:T(8,128)} %constant_dynamic-update-slice_fusion.5, f32[2,1,2,2048,128]{4,3,2,0,1:T(8,128)} %bitcast.42, s32[]{:T(128)S(6)} %select_n.20), kind=kLoop, calls=%fused_computation.29 | loop fusion | bytes 4194308
  171.2 3.1 %constant_dynamic-update-slice_fusion.3 = f32[2,16384,128]{2,1,0:T(8,128)} fusion(f32[2,16384,128]{2,1,0:T(8,128)} %constant_dynamic-update-slice_fusion.4, f32[2,2048,128]{2,1,0:T(8,128)} %collective-permute-done.2), kind=kLoop, calls=%fused_computation.28 | loop fusion | bytes 4194304
  174.3 3.0 %constant_dynamic-update-slice_fusion.2 = f32[2,16384,128]{2,1,0:T(8,128)} fusion(f32[2,16384,128]{2,1,0:T(8,128)} %constant_dynamic-update-slice_fusion.3, f32[2,2048,128]{2,1,0:T(8,128)} %collective-permute-done.1), kind=kLoop, calls=%fused_computation.27 | loop fusion | bytes 4194304
  177.3 1.4 constant_dynamic-update-slice_fusion.1
  178.8 0.0 copy-done.1
  178.8 1.4 constant_dynamic-update-slice_fusion
  180.2 0.0 all-gather.2.cloned.1.call-done
  180.2 0.0 copy-start
  180.2 9.9 %fusion.4 = f32[256,128]{1,0:T(8,128)S(1)} fusion(f32[2,256,8192]{2,1,0:T(8,128)} %all-gather.2.cloned.1.call-done, f32[2,16384,128]{2,1,0:T(8,128)} %constant_dynamic-update-slice_fusion, s32[]{:T(128)S(6)} %select_n.22), kind=kOutput, calls=%fused_computation.4 | convolution fusion | flops 3221225472 | bytes 12713988 | tf_op jit(solution)/shard_map/dot_general | solution.py:17
  190.2 9.8 %fusion.2 = f32[256,128]{1,0:T(8,128)S(1)} fusion(f32[2,256,8192]{2,1,0:T(8,128)} %all-gather.2.cloned.1.call-done, f32[2,16384,128]{2,1,0:T(8,128)} %constant_dynamic-update-slice_fusion, s32[]{:T(128)S(6)} %add.42, s32[]{:T(128)S(6)} %select_n.22), kind=kOutput, calls=%fused_computation.2 | convolution fusion | flops 3221225472 | bytes 12713992 | tf_op jit(solution)/shard_map/dot_general | solution.py:20
  200.0 0.0 copy-done
  200.0 9.6 %fusion.29 = f32[1,256,128]{2,1,0:T(8,128)S(1)} fusion(f32[256,128]{1,0:T(8,128)S(1)} %fusion.2, f32[256,128]{1,0:T(8,128)S(1)} %fusion.4, f32[2,16384,128]{2,1,0:T(8,128)} %constant_dynamic-update-slice_fusion, s32[]{:T(128)S(6)} %select_n.22, s32[]{:T(128)S(6)} %add.42, f32[2,256,8192]{2,1,0:T(8,128)S(1)} %copy-done), kind=kOutput, calls=%fused_computation.22 | convolution fusion | flops 3224436736 | bytes 25559048 | tf_op jit(solution)/shard_map/dot_general | solution.py:23
  209.6 0.7 pad_maximum_fusion
  210.3 0.0 all-reduce.2.cloned.1.call-update
  210.4 21.2 %all-reduce.2.cloned.1.call-done = f32[2,256,128]{2,1,0:T(8,128)} async-done(((f32[2,256,128]{2,1,0:T(8,128)}), f32[2,256,128]{2,1,0:T(8,128)}) %all-reduce.2.cloned.1.call-update) | async-done | bytes 262160 | tf_op jit(solution)/shard_map/psum | solution.py:64
  231.6 1.7 copy.11
  (1 shorter events, 0.0 us)
Async XLA Ops:
  6.5 173.7 %all-gather.2.cloned.1.call-start = ((), (), s32[]{:S(2)}) async-start(), calls=%async_computation | async-start | bytes 20971520 | tf_op jit(solution)/shard_map/all_gather | solution.py:62
  11.3 220.2 %all-reduce.2.cloned.1.call-start = ((), (), s32[]{:S(2)}) async-start(), calls=%async_computation.1 | async-start | bytes 524288 | tf_op jit(solution)/shard_map/psum | solution.py:64
  13.1 50.8 %collective-permute-start = (f32[2,2048,128]{2,1,0:T(8,128)S(1)}, f32[2,2048,128]{2,1,0:T(8,128)S(1)}, u32[]{:S(2)}, u32[]{:S(2)}) collective-permute-start(f32[2,2048,128]{2,1,0:T(8,128)S(1)} %dynamic-slice_bitcast_fusion), channel_id=1, source_target_pairs={{0,4},{4,8},{8,12},{12,0},{1,5},{5,9},{9,13},{13,1},{2,6},{6,10},{... | collective-permute-start | bytes 6291464 | tf_op jit(solution)/shard_map/ppermute | solution.py:57
  63.9 48.7 %collective-permute-start.1 = (f32[2,2048,128]{2,1,0:T(8,128)S(1)}, f32[2,2048,128]{2,1,0:T(8,128)}, u32[]{:S(2)}, u32[]{:S(2)}) collective-permute-start(f32[2,2048,128]{2,1,0:T(8,128)S(1)} %collective-permute-done), channel_id=1, source_target_pairs={{0,4},{4,8},{8,12},{12,0},{1,5},{5,9},{9,13},{13,1},{2,6},{6,10},{... | collective-permute-start | bytes 6291464 | tf_op jit(solution)/shard_map/ppermute | solution.py:57
  112.6 48.1 %collective-permute-start.2 = (f32[2,2048,128]{2,1,0:T(8,128)}, f32[2,2048,128]{2,1,0:T(8,128)}, u32[]{:S(2)}, u32[]{:S(2)}) collective-permute-start(f32[2,2048,128]{2,1,0:T(8,128)} %collective-permute-done.1), channel_id=1, source_target_pairs={{0,4},{4,8},{8,12},{12,0},{1,5},{5,9},{9,13},{13,1},{2,6},{6,10},{... | collective-permute-start | bytes 6291464 | tf_op jit(solution)/shard_map/ppermute | solution.py:57
  112.6 66.2 %copy-start.1 = (f32[2,4096,128]{2,1,0:T(8,128)S(1)}, f32[2,4096,128]{2,1,0:T(8,128)}, u32[]{:S(2)}) copy-start(f32[2,4096,128]{2,1,0:T(8,128)} %param.3) | copy-start | bytes 12582916
  180.2 19.8 %copy-start = (f32[2,256,8192]{2,1,0:T(8,128)S(1)}, f32[2,256,8192]{2,1,0:T(8,128)}, u32[]{:S(2)}) copy-start(f32[2,256,8192]{2,1,0:T(8,128)} %all-gather.2.cloned.1.call-done) | copy-start | bytes 50331652
Sparse Core Ops, SparseCore 0:
  11.4 108.6 all-gather.1
  210.5 21.0 all-reduce.1

commit v2 on v0

--- a/solution.py
+++ b/solution.py
@@ -2,6 +2,7 @@
 import jax.numpy as jnp
 from jax import lax
 from jax.sharding import PartitionSpec as P
+from jax.lax import all_gather
 
 
 def gauss_fold(right_whole, site_rows, cols_out):
@@ -53,7 +54,7 @@
     accumulate, initial = gauss_fold(right_whole, local_rows, local_cols)
     totals = accumulate(initial, lax.all_gather(left_own, "col", axis=2, tiled=True), jnp.int32(0))
     partial_product = combine_terms(totals)
-    product = lax.psum(partial_product, "layer")
+    product = all_gather(partial_product, "layer").sum(axis=0)
     return product
 
 

time: 329 us -> 314 us (0.954)
  waiting for transfers between devices: 277 us -> 253 us
  blocking collectives: 0 us -> 9.12 us
    psum x1 -> x0, waiting for transfers between devices: 23.4 us -> none  [local(): product = lax.psum(partial_product, 'layer')]
    all_gather x0 -> x1, blocking collectives: none -> 9.12 us  [local(): product = all_gather(partial_product, 'layer').sum(axis=0)]
  transfers between devices with their start and end apart: 3 -> 2, of which waited for: 3 -> 2; matrix products, arithmetic and copies ran while one was open for 1% -> 1% of each run, Pallas kernels for 0% -> 0%
where the time goes in v2:
time: 314 us
  waiting for transfers between devices  253 us (81%)
  matrix products  28.9 us (9%)
  between operations  13.5 us (4%)
  blocking collectives  9.12 us (3%)
  local copies, waits for them, and re-layouts  7.7 us (2%)
    all_gather x1, waiting for transfers between devices, local(): right_whole = lax.all_gather(right_own, 'row', axis=1, tiled=True)  148 us
    all_gather x1, waiting for transfers between devices, local(): lax.all_gather(left_own, 'col', axis=2, tiled=True)  106 us
    dot_general x1, matrix products, accumulate(): jnp.dot(left_real, right_real, precision=highest, preferred_element_type=...  9.93 us
    dot_general x1, matrix products, accumulate(): jnp.dot(left_imag, right_imag, precision=highest, preferred_element_type=...  9.8 us
    dot_general x1, matrix products, accumulate(): jnp.dot(left_real + left_imag, right_total, precision=highest, preferred_...  9.2 us
    all_gather x1, blocking collectives, local(): product = all_gather(partial_product, 'layer').sum(axis=0)  9.12 us
  transfers between devices with their start and end apart: 2, of which 2 were waited for; matrix products, arithmetic and copies ran while one was open for 1% of the time, Pallas kernels for 0%

profile of v2, /device:TPU:0, one launch (start us, length us, event | category | flops | bytes accessed | tf_op | source)
XLA Modules:
  0.0 313.5 jit_solution(16335709139186477865)
XLA Ops:
  6.5 0.0 all-gather.7.cloned.1.call-start
  6.5 3.1 constant_dynamic-slice_fusion
  9.6 0.0 all-gather.7.cloned.1.call-update
  9.6 0.0 all-gather.5.cloned.1.call-start
  9.7 4.6 %constant_dynamic-slice_fusion.1 = f32[2,256,2048]{2,1,0:T(8,128)} fusion(f32[2,256,4096]{2,1,0:T(8,128)} %param.2, s32[]{:T(128)S(6)} %select_n.6), kind=kLoop, calls=%fused_computation.25 | loop fusion | bytes 8388612 | tf_op jit(solution)/shard_map/dynamic_slice | solution.py:49
  14.3 0.0 all-gather.5.cloned.1.call-update
  14.3 147.8 %all-gather.7.cloned.1.call-done = f32[2,1,1,8192,128]{4,3,2,0,1:T(8,128)} async-done(((f32[2,1,1,2048,128]{4,3,2,0,1:T(8,128)}), f32[2,1,1,8192,128]{4,3,2,0,1:T(8,128)}) %all-gather.7.cloned.1.call-update) | async-done | bytes 8388624 | tf_op jit(solution)/shard_map/all_gather | solution.py:53
  162.1 105.7 %all-gather.5.cloned.1.call-done = f32[2,256,8192]{2,1,0:T(8,128)} async-done(((f32[2,256,2048]{2,1,0:T(8,128)}), f32[2,256,8192]{2,1,0:T(8,128)}) %all-gather.5.cloned.1.call-update) | async-done | bytes 16777232 | tf_op jit(solution)/shard_map/all_gather | solution.py:55
  267.8 0.0 copy-start
  267.8 9.9 %fusion.4 = f32[256,128]{1,0:T(8,128)S(1)} fusion(f32[2,256,8192]{2,1,0:T(8,128)} %all-gather.5.cloned.1.call-done, f32[2,1,1,8192,128]{4,3,2,0,1:T(8,128)} %all-gather.7.cloned.1.call-done), kind=kOutput, calls=%fused_computation.4 | convolution fusion | flops 3221225472 | bytes 12713984 | tf_op jit(solution)/shard_map/dot_general | solution.py:18
  277.7 9.8 %fusion.2 = f32[256,128]{1,0:T(8,128)S(1)} fusion(f32[2,256,8192]{2,1,0:T(8,128)} %all-gather.5.cloned.1.call-done, f32[2,1,1,8192,128]{4,3,2,0,1:T(8,128)} %all-gather.7.cloned.1.call-done), kind=kOutput, calls=%fused_computation.2 | convolution fusion | flops 3221225472 | bytes 12713984 | tf_op jit(solution)/shard_map/dot_general | solution.py:21
  287.6 0.0 copy-done
  287.6 9.2 %fusion.29 = f32[1,256,128]{2,1,0:T(8,128)S(1)} fusion(f32[256,128]{1,0:T(8,128)S(1)} %fusion.2, f32[256,128]{1,0:T(8,128)S(1)} %fusion.4, f32[2,1,1,8192,128]{4,3,2,0,1:T(8,128)} %all-gather.7.cloned.1.call-done, f32[2,256,8192]{2,1,0:T(8,128)S(1)} %copy-done), kind=kOutput, calls=%fused_computation.21 | convolution fusion | flops 3224436736 | bytes 25559040 | tf_op jit(solution)/shard_map/dot_general | solution.py:24
  296.8 9.1 %all-gather.1 = f32[4,256,128]{2,1,0:T(8,128)S(1)} all-gather(f32[2,256,128]{2,1,0:T(8,128)S(1)} %pad_maximum_fusion), channel_id=3, replica_groups=mesh['layer'=2,'row'=4,'col'=4] {'layer'}, dimensions={0}, use_global_device_ids=true | all-gather | bytes 786432 | tf_op jit(solution)/shard_map/all_gather | solution.py:57
  305.9 0.7 reduce_sum.9
  (2 shorter events, 0.0 us)
Async XLA Ops:
  6.5 155.6 %all-gather.7.cloned.1.call-start = ((), (), s32[]{:S(2)}) async-start(), calls=%async_computation.1 | async-start | bytes 10485760 | tf_op jit(solution)/shard_map/all_gather | solution.py:53
  9.6 258.2 %all-gather.5.cloned.1.call-start = ((), (), s32[]{:S(2)}) async-start(), calls=%async_computation | async-start | bytes 20971520 | tf_op jit(solution)/shard_map/all_gather | solution.py:55
  267.8 19.8 %copy-start = (f32[2,256,8192]{2,1,0:T(8,128)S(1)}, f32[2,256,8192]{2,1,0:T(8,128)}, u32[]{:S(2)}) copy-start(f32[2,256,8192]{2,1,0:T(8,128)} %all-gather.5.cloned.1.call-done) | copy-start | bytes 50331652
Sparse Core Ops, SparseCore 0:
  9.7 152.3 all-gather.6
  163.7 104.0 all-gather.4
